TPU v7x, 32 devices: a whole 2x2x4 slice. The times are simulated.
32 devices in a mesh: blk: 8 (over z, x), col: 4 (over y, core).
Axes of the slice: x: 2, y: 2, z: 4, core: 2. Of those that a mesh axis runs over, the one named last changes fastest.
Arguments:
- momentum: float32 [2048, 29568], P('blk', 'col'), may hold values from -200 to 200
- grad: bfloat16 [2048, 29568], P('blk', 'col'), may hold values from -6 to 6
- q_basis: bfloat16 [1024, 29568], P('blk', 'col'), may hold values from -6 to 6
Outputs:
- momentum_new: float32 [2048, 29568], P('blk', 'col')
- update: bfloat16 [2048, 29568], P('blk', 'col')
- q_new: bfloat16 [1024, 29568], P('blk', 'col')
All inputs are finite; a program needn't handle non-finite values.
Results may differ from a plain program's by a relative error of at most 0.022.
Values may be sent and summed in bfloat16 or wider, within the bound.
A program may use at most 128 MiB of HBM per device.

v0:
```python
import jax
import jax.numpy as jnp
from jax import lax
from jax.sharding import PartitionSpec as P

decay_rest = 0.05
epsilon = 1e-06


def shards(momentum, grad, q_basis):
    b_matrix = momentum + grad.astype(jnp.float32)
    b_half = b_matrix.astype(jnp.bfloat16)
    rows_total = b_half.shape[0] * lax.axis_size("blk")
    feature_count = b_half.shape[1] * lax.axis_size("col")
    k_local = q_basis.shape[0]
    p_partial = lax.dot_general(
        b_half,
        lax.all_gather(q_basis, "blk", axis=0, tiled=True),
        (((1,), (1,)), ((), ())),
        preferred_element_type=jnp.float32,
    )
    p_matrix = lax.psum(p_partial.astype(jnp.bfloat16), "col").astype(jnp.float32)
    squares = lax.psum(jnp.sum(p_matrix * p_matrix, axis=0), "blk")
    p_hat = (p_matrix / jnp.sqrt(squares / rows_total + epsilon)[None, :]).astype(jnp.bfloat16)
    rank_count = p_hat.shape[1]
    r_partial = lax.dot_general(
        p_hat, b_half, (((0,), (0,)), ((), ())), preferred_element_type=jnp.float32
    )
    r_matrix = lax.psum(r_partial.astype(jnp.bfloat16), "blk").astype(jnp.float32)
    squares_r = lax.psum(jnp.sum(r_matrix * r_matrix, axis=1), "col")
    r_scale = jnp.sqrt(squares_r / feature_count + epsilon)
    q_full = (r_matrix / r_scale[:, None]).astype(jnp.bfloat16)
    weighted = (p_hat.astype(jnp.float32) * (decay_rest * r_scale / rows_total)[None, :]).astype(
        jnp.bfloat16
    )
    update_sum = jnp.dot(p_hat, q_full, preferred_element_type=jnp.float32)
    correction = jnp.dot(weighted, q_full, preferred_element_type=jnp.float32)
    q_new = lax.dynamic_slice_in_dim(q_full, lax.axis_index("blk") * k_local, k_local, 0)
    update = (update_sum * (1.0 / jnp.sqrt(jnp.float32(rank_count)))).astype(jnp.bfloat16)
    return (b_matrix - correction, update, q_new)


def solution(mesh):
    in_specs = (P("blk", "col"), P("blk", "col"), P("blk", "col"))
    out_specs = (P("blk", "col"), P("blk", "col"), P("blk", "col"))
    return jax.shard_map(shards, mesh=mesh, in_specs=in_specs, out_specs=out_specs, check_vma=False)
```

profile of v0, /device:TPU:0, one launch (start us, length us, event | category | flops | bytes accessed | tf_op | source)
XLA Modules:
  0.0 824.6 jit_solution(4238878799680030414)
XLA Ops:
  7.2 0.0 all-gather.2.cloned.1.call-start
  7.2 0.7 all-gather.2.cloned.1.call-update
  7.9 0.0 all-reduce.3.cloned.1.call-start
  7.9 212.1 %all-gather.2.cloned.1.call-done = bf16[1024,7392]{0,1:T(8,128)(2,1)} async-done(((bf16[128,7392]{0,1:T(8,128)(2,1)}), bf16[1024,7392]{0,1:T(8,128)(2,1)}) %all-gather.2.cloned.1.call-update) | async-done | bytes 15138832 | tf_op jit(solution)/shard_map/all_gather | solution.py:18
  220.1 13.5 %convolution_convert_fusion.1 = bf16[256,1024]{1,0:T(8,128)(2,1)} fusion(bf16[1024,7392]{0,1:T(8,128)(2,1)} %all-gather.2.cloned.1.call-done, f32[256,7392]{0,1:T(8,128)} %param.3, bf16[256,7392]{0,1:T(8,128)(2,1)} %param.4), kind=kOutput, calls=%fused_computation.12 | convolution fusion | flops 3881476096 | bytes 27017216 | tf_op jit(solution)/shard_map/dot_general | solution.py:16
  233.6 0.0 all-reduce.3.cloned.1.call-update
  233.6 0.0 all-reduce.5.cloned.1.call-start
  233.7 31.7 %all-reduce.3.cloned.1.call-done = bf16[256,1024]{1,0:T(8,128)(2,1)} async-done(((bf16[256,1024]{1,0:T(8,128)(2,1)}), bf16[256,1024]{1,0:T(8,128)(2,1)}) %all-reduce.3.cloned.1.call-update) | async-done | bytes 524304 | tf_op jit(solution)/shard_map/psum | solution.py:22
  265.3 1.2 fusion.4
  266.5 21.4 %psum.29 = f32[1024]{0:T(1024)S(1)} all-reduce(f32[1024]{0:T(1024)S(1)} %fusion.4), channel_id=1, replica_groups=mesh['blk'=8,'col'=4] {'blk'}, use_global_device_ids=true, to_apply=%region_2.0 | all-reduce | flops 1024 | bytes 8192 | tf_op jit(solution)/shard_map/psum | solution.py:23
  287.9 13.8 %convolution_convert_fusion = bf16[1024,7392]{0,1:T(8,128)(2,1)} fusion(f32[256,7392]{0,1:T(8,128)} %param.3, bf16[256,7392]{0,1:T(8,128)(2,1)} %param.4, bf16[256,1024]{1,0:T(8,128)(2,1)} %all-reduce.3.cloned.1.call-done, f32[1024]{0:T(1024)S(1)} %add_sqrt_fusion.1), kind=kOutput, calls=%fused_computation.4 | convolution fusion | flops 3889569792 | bytes 27021312 | tf_op jit(solution)/shard_map/dot_general | solution.py:26
  301.7 0.0 all-reduce.5.cloned.1.call-update
  301.7 461.4 %all-reduce.5.cloned.1.call-done = bf16[1024,7392]{0,1:T(8,128)(2,1)} async-done(((bf16[1024,7392]{0,1:T(8,128)(2,1)}), bf16[1024,7392]{0,1:T(8,128)(2,1)}) %all-reduce.5.cloned.1.call-update) | async-done | bytes 15138832 | tf_op jit(solution)/shard_map/psum | solution.py:29
  763.1 8.3 %fusion = f32[1024]{0:T(1024)S(1)} fusion(bf16[1024,7392]{0,1:T(8,128)(2,1)} %all-reduce.5.cloned.1.call-done), kind=kLoop, calls=%fused_computation.2 | loop fusion | flops 22707200 | bytes 15142912 | tf_op jit(solution)/shard_map/reduce_sum | solution.py:30
  771.4 6.4 psum.31
  777.8 0.0 copy-start.2
  777.8 9.0 %fusion.1 = bf16[1024,7392]{0,1:T(8,128)(2,1)S(1)} fusion(bf16[1024,7392]{0,1:T(8,128)(2,1)} %all-reduce.5.cloned.1.call-done, f32[1024]{0:T(1024)S(1)} %get-tuple-element.4), kind=kLoop, calls=%fused_computation.3 | loop fusion | flops 22708224 | bytes 30281728 | tf_op jit(solution)/shard_map/convert_element_type | solution.py:32
  786.9 0.0 copy-start
  786.9 5.3 copy-done
  792.2 0.0 slice-start
  792.2 1.7 constant_dynamic-slice_fusion
  794.0 0.0 copy-done.2
  794.0 0.0 slice-start.1
  794.0 0.0 copy-start.1
  794.0 11.5 %fusion.2 = bf16[256,7392]{0,1:T(8,128)(2,1)} fusion(bf16[1024,7392]{0,1:T(8,128)(2,1)} %copy-done, bf16[256,1024]{1,0:T(8,128)(2,1)S(1)} %copy-done.2, f32[1024]{0:T(1024)S(1)} %add_sqrt_fusion.1), kind=kOutput, calls=%fused_computation.7 | convolution fusion | flops 3880108032 | bytes 19451904 | tf_op jit(solution)/shard_map/dot_general | solution.py:36
  805.5 0.0 slice-done
  805.5 0.0 slice-done.1
  805.5 0.0 copy-done.1
  805.5 12.6 %convolution_subtract_fusion = f32[256,7392]{0,1:T(8,128)} fusion(bf16[1024,7392]{0,1:T(8,128)(2,1)} %copy-done, f32[256,7392]{0,1:T(8,128)S(1)} %bitcast.4, bf16[256,7392]{0,1:T(8,128)(2,1)S(1)} %copy-done.1, f32[1024]{0:T(1024)S(1)} %get-tuple-element.3, bf16[256,1024]{1,0:T(8,128)(2,1)S(1)} %copy-done.2, f32[1024]{0:T(1024)S(1)} %add_sqrt_fusion.1), kind=kOutput, calls=%fused_computation.6 | convolution fusion | flops 3882786816 | bytes 34594816 | tf_op jit(solution)/shard_map/dot_general | solution.py:37
  (3 shorter events, 0.0 us)
Async XLA Ops:
  7.2 212.9 %all-gather.2.cloned.1.call-start = ((), (), s32[]{:S(2)}) async-start(), calls=%async_computation | async-start | bytes 17031168 | tf_op jit(solution)/shard_map/all_gather | solution.py:18
  7.9 257.4 %all-reduce.3.cloned.1.call-start = ((), (), s32[]{:S(2)}) async-start(), calls=%async_computation.1 | async-start | bytes 1048576 | tf_op jit(solution)/shard_map/psum | solution.py:22
  233.6 529.5 %all-reduce.5.cloned.1.call-start = ((), (), s32[]{:S(2)}) async-start(), calls=%async_computation.2 | async-start | bytes 30277632 | tf_op jit(solution)/shard_map/psum | solution.py:29
  777.8 16.1 %copy-start.2 = (bf16[256,1024]{1,0:T(8,128)(2,1)S(1)}, bf16[256,1024]{1,0:T(8,128)(2,1)}, u32[]{:S(2)}) copy-start(bf16[256,1024]{1,0:T(8,128)(2,1)} %all-reduce.3.cloned.1.call-done) | copy-start | bytes 1572868
  786.9 5.3 copy-start
  792.2 13.3 %slice-start = ((s8[7569408]{0:T(1024)(128)(4,1)}), s8[4194304]{0:T(1024)(128)(4,1)S(1)}, s32[]{:S(2)}) async-start(s8[7569408]{0:T(1024)(128)(4,1)} %bitcast.3), calls=%async_computation.3 | async-start | bytes 8388608
  794.0 11.5 %slice-start.1 = ((s8[7569408]{0:T(1024)(128)(4,1)}), s8[3375104]{0:T(1024)(128)(4,1)S(1)}, s32[]{:S(2)}) async-start(s8[7569408]{0:T(1024)(128)(4,1)} %bitcast.3), calls=%async_computation.4 | async-start | bytes 6750208
  794.0 11.5 %copy-start.1 = (bf16[256,7392]{0,1:T(8,128)(2,1)S(1)}, bf16[256,7392]{0,1:T(8,128)(2,1)}, u32[]{:S(2)}) copy-start(bf16[256,7392]{0,1:T(8,128)(2,1)} %param.4) | copy-start | bytes 11354116
Sparse Core Ops, SparseCore 0:
  10.0 210.0 all-gather.1
  233.7 31.5 all-reduce.2
  301.8 461.2 all-reduce.4
where the time goes:
time: 825 us
  waiting for transfers between devices  706 us (86%)
  matrix products  51.4 us (6%)
  blocking collectives  27.8 us (3%)
  other arithmetic  18.5 us (2%)
  between operations  13.8 us (2%)
    psum x1, waiting for transfers between devices, shards(): lax.psum(r_partial.astype(jnp.bfloat16), 'blk').astype(jnp.float32)  461 us
    all_gather x1, waiting for transfers between devices, shards(): lax.all_gather(q_basis, 'blk', axis=0, tiled=True)  212 us
    psum x1, waiting for transfers between devices, shards(): lax.psum(p_partial.astype(jnp.bfloat16), 'col').astype(jnp.float32)  31.7 us
    psum x1, blocking collectives, shards(): squares = lax.psum(jnp.sum(p_matrix * p_matrix, axis=0), 'blk')  21.4 us
  transfers between devices with their start and end apart: 3, of which 3 were waited for; matrix products, arithmetic and copies ran while one was open for 0% of the time, Pallas kernels for 0%

commit v1 on v0

v1 whole, which is shorter than its diff:
```python
import functools

import jax
import jax.numpy as jnp
from jax import lax
from jax.experimental import pallas as pl
from jax.experimental.pallas import tpu as pltpu
from jax.sharding import PartitionSpec as P

MESH = pl.DeviceIdType.MESH
decay_rest = 0.05
epsilon = 1e-06
LANES = 128
PARAMS = functools.partial(pltpu.CompilerParams, has_side_effects=True, vmem_limit_bytes=60 * 1024 * 1024)


def greet(peers):
    barrier = pltpu.get_barrier_semaphore()
    for peer in peers:
        pl.semaphore_signal(barrier, inc=1, device_id=peer, device_id_type=MESH)
    pl.semaphore_wait(barrier, len(peers))


def remote(src, dst, send, recv, peer):
    return pltpu.make_async_remote_copy(
        src_ref=src, dst_ref=dst, send_sem=send, recv_sem=recv, device_id=peer, device_id_type=MESH
    )


def spread_kernel(n_out, n_in, b_ref, q_ref, bz_ref, qf_ref, b_own, q_own, own_sem, sb, rb, sq, rq, sf, rf):
    blk, col = lax.axis_index("blk"), lax.axis_index("col")
    me_o, me_i = blk // n_in, lax.rem(blk, n_in)
    outer = [lax.rem(me_o + k, n_out) for k in range(n_out)]
    width = bz_ref.shape[-1]
    wide = [pl.ds(pl.multiple_of(o * width, LANES), width) for o in outer]
    inner = [lax.rem(me_i + k, n_in) for k in range(n_in)]
    greet(
        [(outer[k] * n_in + me_i, col) for k in range(1, n_out)]
        + [(me_o * n_in + inner[j], col) for j in range(1, n_in)]
    )
    load_b = pltpu.make_async_copy(b_ref.at[:, wide[0]], b_own, own_sem.at[0])
    load_q = pltpu.make_async_copy(q_ref.at[:, wide[0]], q_own, own_sem.at[1])
    load_b.start()
    load_q.start()
    q_sends, b_sends, forwards = [], [], []
    for k in range(1, n_out):
        peer = (outer[k] * n_in + me_i, col)
        copy = remote(q_ref.at[:, wide[k]], qf_ref.at[me_o, me_i], sq.at[k], rq.at[k], peer)
        copy.start()
        q_sends.append(copy)
    for j in range(1, n_in):
        peer = (me_o * n_in + inner[j], col)
        copy = remote(q_ref.at[:, wide[0]], qf_ref.at[me_o, me_i], sf.at[j, 0], rf.at[j, 0], peer)
        copy.start()
        forwards.append(copy)
    for k in range(1, n_out):
        peer = (outer[k] * n_in + me_i, col)
        copy = remote(b_ref.at[:, wide[k]], bz_ref.at[me_o], sb.at[k], rb.at[k], peer)
        copy.start()
        b_sends.append(copy)
    load_b.wait()
    load_q.wait()
    store_b = pltpu.make_async_copy(b_own, bz_ref.at[me_o], own_sem.at[0])
    store_q = pltpu.make_async_copy(q_own, qf_ref.at[me_o, me_i], own_sem.at[1])
    store_b.start()
    store_q.start()
    for k in range(1, n_out):
        q_sends[k - 1].wait_recv()
        came_from = lax.rem(me_o + n_out - k, n_out)
        for j in range(1, n_in):
            peer = (me_o * n_in + inner[j], col)
            piece = qf_ref.at[came_from, me_i]
            copy = remote(piece, piece, sf.at[j, k], rf.at[j, k], peer)
            copy.start()
            forwards.append(copy)
    for copy in q_sends:
        copy.wait_send()
    for copy in b_sends + forwards:
        copy.wait()
    store_b.wait()
    store_q.wait()


def spread(n_out, n_in, b_half, q_basis):
    width = b_half.shape[1] // n_out
    b_part = (b_half.shape[0], width)
    q_part = (q_basis.shape[0], width)
    any_space = pl.BlockSpec(memory_space=pl.ANY)
    dma = pltpu.SemaphoreType.DMA
    return pl.pallas_call(
        functools.partial(spread_kernel, n_out, n_in),
        out_shape=(
            jax.ShapeDtypeStruct((n_out,) + b_part, b_half.dtype),
            jax.ShapeDtypeStruct((n_out, n_in) + q_part, q_basis.dtype),
        ),
        in_specs=[any_space] * 2,
        out_specs=(any_space, any_space),
        scratch_shapes=[
            pltpu.VMEM(b_part, b_half.dtype),
            pltpu.VMEM(q_part, q_basis.dtype),
            dma((2,)),
            dma((n_out,)),
            dma((n_out,)),
            dma((n_out,)),
            dma((n_out,)),
            dma((n_in, n_out)),
            dma((n_in, n_out)),
        ],
        compiler_params=PARAMS(collective_id=0),
        name="spread",
    )(b_half, q_basis)


def left_kernel(
    n_out, n_in, n_col, n_core, rows_total, pt_ref, out_ref,
    half, summed, got, squares, squares_got, mine, s0, r0, s1, r1, s2, r2, s3, r3, s4, r4, own_sem
):
    blk, col = lax.axis_index("blk"), lax.axis_index("col")
    me_o, me_i = blk // n_in, lax.rem(blk, n_in)
    n_chip = n_col // n_core
    chip, core = col // n_core, lax.rem(col, n_core)
    members = n_out * n_chip
    me = me_o * n_chip + chip
    place, peers, source = [], [], []
    for k in range(members):
        g = lax.rem(me + k, members)
        place.append(g)
        peers.append(((g // n_chip) * n_in + me_i, lax.rem(g, n_chip) * n_core + core))
        source.append(lax.rem(me + members - k, members))
    inner_peers = [(me_o * n_in + lax.rem(me_i + j, n_in), col) for j in range(n_in)]
    cores = [lax.rem(core + j, n_core) for j in range(n_core)]
    core_peers = [(blk, chip * n_core + cores[j]) for j in range(n_core)]
    greet(peers[1:] + inner_peers[1:] + core_peers[1:])
    hand = []
    for j in range(1, n_core):
        copy = remote(pt_ref.at[cores[j]], half.at[j], s0.at[j], r0.at[j], core_peers[j])
        copy.start()
        hand.append(copy)
    for copy in hand:
        copy.wait_recv()

    def add_cores(g):
        total = pt_ref[core, g].astype(jnp.float32)
        for j in range(1, n_core):
            total = total + half[j, g].astype(jnp.float32)
        return total

    sends = []
    for k in list(range(1, members)) + [0]:
        summed[place[k]] = add_cores(place[k]).astype(summed.dtype)
        if k:
            copy = remote(summed.at[place[k]], got.at[k], s1.at[k], r1.at[k], peers[k])
            copy.start()
            sends.append(copy)
    total = add_cores(me)
    for k in range(1, members):
        sends[k - 1].wait_recv()
        total = total + got[k].astype(jnp.float32)
    square = jnp.sum(total * total, axis=1, keepdims=True)
    squares[...] = jnp.broadcast_to(square, squares.shape)
    swaps = []
    for j in range(1, n_in):
        copy = remote(squares, squares_got.at[j], s2.at[j], r2.at[j], inner_peers[j])
        copy.start()
        swaps.append(copy)
    full = squares[...]
    for j in range(1, n_in):
        swaps[j - 1].wait_recv()
        full = full + squares_got[j]
    scale = jnp.sqrt(full[:, :1] / rows_total + epsilon)
    mine[...] = (total / scale).astype(mine.dtype)
    own = pltpu.make_async_copy(mine, out_ref.at[core, me], own_sem.at[0])
    own.start()
    gathers, passes = [], []
    for k in range(1, members):
        copy = remote(mine, out_ref.at[core, me], s3.at[k], r3.at[k], peers[k])
        copy.start()
        gathers.append(copy)
    for j in range(1, n_core):
        copy = remote(mine, out_ref.at[core, me], s4.at[j, 0], r4.at[j, 0], core_peers[j])
        copy.start()
        passes.append(copy)
    for k in range(1, members):
        gathers[k - 1].wait_recv()
        for j in range(1, n_core):
            piece = out_ref.at[core, source[k]]
            copy = remote(piece, piece, s4.at[j, k], r4.at[j, k], core_peers[j])
            copy.start()
            passes.append(copy)
    for copy in hand + sends + swaps + gathers:
        copy.wait_send()
    for copy in passes:
        copy.wait()
    own.wait()


def left(n_out, n_in, n_col, rows_total, pt):
    n_core = 2 if n_col % 2 == 0 else 1
    members = n_out * n_col // n_core
    rank, rows = pt.shape
    part = rank // (members * n_core)
    dma = pltpu.SemaphoreType.DMA
    vmem = pl.BlockSpec(memory_space=pltpu.VMEM)
    shape = (n_core, members, part, rows)
    out = pl.pallas_call(
        functools.partial(left_kernel, n_out, n_in, n_col, n_core, rows_total),
        out_shape=jax.ShapeDtypeStruct(shape, pt.dtype),
        in_specs=[vmem],
        out_specs=vmem,
        scratch_shapes=[
            pltpu.VMEM(shape, pt.dtype),
            pltpu.VMEM((members, part, rows), pt.dtype),
            pltpu.VMEM((members, part, rows), pt.dtype),
            pltpu.VMEM((part, LANES), jnp.float32),
            pltpu.VMEM((n_in, part, LANES), jnp.float32),
            pltpu.VMEM((part, rows), pt.dtype),
        ]
        + [dma((n_core,))] * 2
        + [dma((members,))] * 2
        + [dma((n_in,))] * 2
        + [dma((members,))] * 2
        + [dma((n_core, members))] * 2
        + [dma((1,))],
        compiler_params=PARAMS(collective_id=1),
        name="left",
    )(pt.reshape(shape))
    return out.reshape(rank, rows)


def right_kernel(
    n_out, n_in, n_col, r_ref, full_ref, sum_ref,
    got, mine, squares, squares_got, s1, r1, sz, rz, sx, rx, s2, r2, s3, r3, own_sem
):
    blk, col = lax.axis_index("blk"), lax.axis_index("col")
    me_o, me_i = blk // n_in, lax.rem(blk, n_in)
    width = r_ref.shape[-1]
    inner = [lax.rem(me_i + j, n_in) for j in range(n_in)]
    origin = [lax.rem(me_i + n_in - j, n_in) for j in range(n_in)]
    peers = [(me_o * n_in + inner[j], col) for j in range(n_in)]
    members = n_out * n_col
    mates = []
    for k in range(members):
        g = lax.rem(me_o * n_col + col + k, members)
        mates.append(((g // n_col) * n_in + me_i, lax.rem(g, n_col)))
    greet(peers[1:] + mates[1:])
    first = list(range(n_out // 2))

    def slot(p, i, o):
        return full_ref.at[p, i, :, pl.ds(pl.multiple_of(o * width, LANES), width)]

    def along(way, s, p, d, source, piece):
        peer = ((me_o + 1 if way == 0 else me_o - 1) * n_in + me_i, col)
        return remote(source, piece, sz.at[way, s, p, d], rz.at[way, s, p, d], peer)

    def can_send(way):
        return me_o < n_out - 1 if way == 0 else me_o > 0

    def came(way, d):
        return (me_o - d, me_o >= d) if way == 0 else (me_o + d, me_o + d < n_out)

    def across(j, p, index, source, piece):
        return remote(source, piece, sx.at[j, p, index], rx.at[j, p, index], peers[j])

    def mark(way, d):
        return d if way == 0 else n_out - 1 + d

    sends = {}
    for p in range(n_out):
        for j in range(1, n_in):
            copy = remote(r_ref.at[p, inner[j]], got.at[j, p], s1.at[j, p], r1.at[j, p], peers[j])
            copy.start()
            sends[j, p] = copy
    squares[...] = jnp.zeros_like(squares)
    ones = jnp.ones((8, width), jnp.float32)
    for p in range(n_out):
        for j in range(1, n_in):
            sends[j, p].wait_recv()
        total = r_ref[p, me_i].astype(jnp.float32)
        for j in range(1, n_in):
            total = total + got[j, p].astype(jnp.float32)
        mine[p] = total.astype(mine.dtype)
        squares[p] = lax.dot_general(
            ones, total * total, (((1,), (1,)), ((), ())),
            precision=lax.Precision.HIGHEST, preferred_element_type=jnp.float32,
        )
        own = slot(p, me_i, me_o)
        pltpu.make_async_copy(mine.at[p], own, own_sem.at[p]).start()
        for j in range(1, n_in):
            across(j, p, 0, mine.at[p], own).start()
        for way in range(2):
            @pl.when(can_send(way))
            def _():
                along(way, 0, p, 1, mine.at[p], own).start()
    pooled = []
    for k in range(1, members):
        copy = remote(squares, squares_got.at[k], s2.at[k], r2.at[k], mates[k])
        copy.start()
        pooled.append(copy)
    for p in first:
        for j in range(1, n_in):
            piece = slot(p, origin[j], me_o)
            across(j, p, 0, piece, piece).wait_recv()
            for way in range(2):
                @pl.when(can_send(way))
                def _():
                    along(way, j, p, 1, piece, piece).start()
    for d in range(1, n_out):
        for p in list(range(len(first), n_out)) + first:
            for s in range(n_in if p in first else 1):
                for way in range(2):
                    o, there = came(way, d)

                    @pl.when(there)
                    def _():
                        piece = slot(p, origin[s], o)
                        along(way, s, p, d, piece, piece).wait_recv()
                        if d < n_out - 1:
                            @pl.when(can_send(way))
                            def _():
                                along(way, s, p, d + 1, piece, piece).start()
                        if p not in first:
                            for j in range(1, n_in):
                                across(j, p, mark(way, d), piece, piece).start()
    total = squares[...]
    for k in range(1, members):
        pooled[k - 1].wait_recv()
        total = total + squares_got[k]
    sum_ref[0] = total
    swaps = []
    for j in range(1, n_in):
        copy = remote(sum_ref.at[0], sum_ref.at[j], s3.at[j], r3.at[j], peers[j])
        copy.start()
        swaps.append(copy)
    for p in range(n_out):
        own = slot(p, me_i, me_o)
        pltpu.make_async_copy(mine.at[p], own, own_sem.at[p]).wait()
        for j in range(1, n_in):
            across(j, p, 0, mine.at[p], own).wait_send()
            if p not in first:
                piece = slot(p, origin[j], me_o)
                across(j, p, 0, piece, piece).wait_recv()
        for s in range(n_in if p in first else 1):
            for way in range(2):
                for d in range(1, n_out):
                    o, there = came(way, d - 1)

                    @pl.when(there & can_send(way))
                    def _():
                        piece = slot(p, origin[s], o)
                        along(way, s, p, d, piece, piece).wait_send()
        if p not in first:
            for way in range(2):
                for d in range(1, n_out):
                    o, there = came(way, d)

                    @pl.when(there)
                    def _():
                        for j in range(1, n_in):
                            mark_at = mark(way, d)
                            piece = slot(p, me_i, o)
                            across(j, p, mark_at, piece, piece).wait_send()
                            piece = slot(p, origin[j], o)
                            across(j, p, mark_at, piece, piece).wait_recv()
    for copy in list(sends.values()) + pooled:
        copy.wait_send()
    for copy in swaps:
        copy.wait()


def right(n_out, n_in, n_col, r):
    rank, width = r.shape
    part = rank // (n_out * n_in)
    members = n_out * n_col
    dma = pltpu.SemaphoreType.DMA
    vmem = pl.BlockSpec(memory_space=pltpu.VMEM)
    full, sums = pl.pallas_call(
        functools.partial(right_kernel, n_out, n_in, n_col),
        out_shape=(
            jax.ShapeDtypeStruct((n_out, n_in, part, n_out * width), r.dtype),
            jax.ShapeDtypeStruct((n_in, n_out, 8, part), jnp.float32),
        ),
        in_specs=[vmem],
        out_specs=(pl.BlockSpec(memory_space=pl.ANY), vmem),
        scratch_shapes=[
            pltpu.VMEM((n_in, n_out, part, width), r.dtype),
            pltpu.VMEM((n_out, part, width), r.dtype),
            pltpu.VMEM((n_out, 8, part), jnp.float32),
            pltpu.VMEM((members, n_out, 8, part), jnp.float32),
        ]
        + [dma((n_in, n_out))] * 2
        + [dma((2, n_in, n_out, n_out))] * 2
        + [dma((n_in, n_out, 2 * n_out - 1))] * 2
        + [dma((members,))] * 2
        + [dma((n_in,))] * 2
        + [dma((n_out,))],
        compiler_params=PARAMS(collective_id=2),
        name="right",
    )(r.reshape(n_out, n_in, part, width))
    me_i = lax.rem(lax.axis_index("blk"), n_in)
    order = lax.rem(me_i - jnp.arange(n_in) + n_in, n_in)
    sums = jnp.take(sums[:, :, 0, :], order, axis=0).transpose(1, 0, 2).reshape(rank)
    return full.reshape(rank, n_out * width), sums


def shards(n_blk, n_col, momentum, grad, q_basis):
    n_out = 4 if n_blk % 4 == 0 else n_blk
    n_in = n_blk // n_out
    rows, cols = momentum.shape
    rank_rows = q_basis.shape[0]
    rank = rank_rows * n_blk
    rows_total, feature_count = rows * n_blk, cols * n_col
    width = -(-cols // (n_out * LANES)) * LANES
    pad = ((0, 0), (0, n_out * width - cols))

    b_matrix = momentum + grad.astype(jnp.float32)
    bz, qf = spread(n_out, n_in, jnp.pad(b_matrix.astype(jnp.bfloat16), pad), jnp.pad(q_basis, pad))
    bz = bz.reshape(n_out * rows, width)
    qf = qf.reshape(rank, width)
    pt = lax.dot_general(qf, bz, (((1,), (1,)), ((), ())), preferred_element_type=jnp.float32)
    p_hat_t = left(n_out, n_in, n_col, rows_total, pt.astype(jnp.bfloat16))
    r_part = jnp.dot(p_hat_t, bz, preferred_element_type=jnp.float32).astype(jnp.bfloat16)
    r_sum, squares = right(n_out, n_in, n_col, r_part)
    r_scale = jnp.sqrt(squares / feature_count + epsilon)
    blk = lax.axis_index("blk")
    p_mine = lax.dynamic_slice_in_dim(p_hat_t, (blk // n_in) * rows, rows, 1)
    p_even = (p_mine.astype(jnp.float32) / r_scale[:, None]).astype(jnp.bfloat16)
    over = (((0,), (0,)), ((), ()))
    correction = lax.dot_general(p_mine, r_sum, over, preferred_element_type=jnp.float32)[:, :cols]
    update = lax.dot_general(p_even, r_sum, over, preferred_element_type=jnp.float32)[:, :cols]
    update = (update * (1.0 / jnp.sqrt(jnp.float32(rank)))).astype(jnp.bfloat16)
    start = blk * rank_rows
    r_mine = lax.dynamic_slice_in_dim(r_sum, start, rank_rows, 0)[:, :cols].astype(jnp.float32)
    scale_mine = lax.dynamic_slice_in_dim(r_scale, start, rank_rows, 0)
    q_new = (r_mine / scale_mine[:, None]).astype(jnp.bfloat16)
    return (b_matrix - correction * (decay_rest / rows_total), update, q_new)


def solution(mesh):
    in_specs = (P("blk", "col"), P("blk", "col"), P("blk", "col"))
    out_specs = (P("blk", "col"), P("blk", "col"), P("blk", "col"))
    body = functools.partial(shards, mesh.shape["blk"], mesh.shape["col"])
    return jax.shard_map(body, mesh=mesh, in_specs=in_specs, out_specs=out_specs, check_vma=False)
```

time: 825 us -> 507 us (0.61)
  waiting for transfers between devices: 706 us -> 0 us
  Pallas kernels: 0 us -> 415 us
  local copies, waits for them, and re-layouts: 7.09 us -> 35.4 us
  blocking collectives: 27.8 us -> 0 us
  between operations: 13.8 us -> 0.73 us
  other arithmetic: 18.5 us -> 8.12 us
    psum x2 -> x0, waiting for transfers between devices: 493 us -> none  [the longest x1 461 us: shards(): lax.psum(r_partial.astype(jnp.bfloat16), 'blk').astype(jnp.float32)]
    pallas_call x0 -> x3, Pallas kernels: none -> 415 us  [the longest x1 233 us: right(): pl.pallas_call(functools.partial(right_kernel, n_out, n_in, n_col), out_s...]
    all_gather x1 -> x0, waiting for transfers between devices: 212 us -> none  [shards(): lax.all_gather(q_basis, 'blk', axis=0, tiled=True)]
    psum x2 -> x0, blocking collectives: 27.8 us -> none  [the longest x1 21.4 us: shards(): squares = lax.psum(jnp.sum(p_matrix * p_matrix, axis=0), 'blk')]
    unnamed x10 -> x9, local copies, waits for them, and re-layouts: 5.35 us -> 28.7 us
    reduce_sum x2 -> x0, other arithmetic: 9.47 us -> none  [the longest x1 8.3 us: shards(): squares_r = lax.psum(jnp.sum(r_matrix * r_matrix, axis=1), 'col')]
  transfers between devices with their start and end apart: 3 -> 0, of which waited for: 3 -> 0; matrix products, arithmetic and copies ran while one was open for 0% -> 0% of each run, Pallas kernels for 0% -> 0%
where the time goes in v1:
time: 507 us; the launch traced here: 506 us
  Pallas kernels  415 us (82%)
  matrix products  46.3 us (9%)
  local copies, waits for them, and re-layouts  35.4 us (7%)
  other arithmetic  8.12 us (2%)
    pallas_call x1, Pallas kernels, right(): pl.pallas_call(functools.partial(right_kernel, n_out, n_in, n_col), out_s...  233 us
    pallas_call x1, Pallas kernels, spread(): pl.pallas_call(functools.partial(spread_kernel, n_out, n_in), out_shape=(...  113 us
    pallas_call x1, Pallas kernels, left(): pl.pallas_call(functools.partial(left_kernel, n_out, n_in, n_col, n_core,...  69.6 us
    unnamed x9, local copies, waits for them, and re-layouts  28.7 us
    dot_general x1, matrix products, shards(): lax.dot_general(p_mine, r_sum, over, preferred_element_type=jnp.float32)  16.3 us
    dot_general x1, matrix products, shards(): lax.dot_general(p_even, r_sum, over, preferred_element_type=jnp.float32)  13.4 us

profile of v1, /device:TPU:0, one launch (start us, length us, event | category | flops | bytes accessed | tf_op | source)
XLA Modules:
  0.0 505.8 jit_solution(7637465691813888313)
XLA Ops:
  0.6 8.7 %copy.13 = f32[256,7392]{1,0:T(8,128)} copy(f32[256,7392]{0,1:T(8,128)} %param.3) | data formatting | bytes 15138816 | tf_op args[0]
  9.4 6.2 %copy.12 = bf16[256,7392]{1,0:T(8,128)(2,1)} copy(bf16[256,7392]{0,1:T(8,128)(2,1)} %param.4) | data formatting | bytes 7569408 | tf_op args[1]
  15.5 4.9 fusion.16
  20.4 2.2 pad.8.b_ref
  22.6 2.8 copy.14
  25.4 1.4 pad.9.q_ref
  26.8 113.1 %spread.1 = (bf16[4,256,1920]{2,1,0:T(8,128)(2,1)}, bf16[4,2,128,1920]{3,2,1,0:T(8,128)(2,1)}) custom-call(bf16[256,7680]{1,0:T(8,128)(2,1)} %pad.8.b_ref, bf16[128,7680]{1,0:T(8,128)(2,1)} %pad.9.q_ref), custom_call_target="tpu_custom_call" | custom-call | tf_op jit(solution)/shard_map/spread/pallas_call | solution.py:90
  139.9 9.1 %convolution_convert_fusion.1 = bf16[1024,1024]{1,0:T(8,128)(2,1)} fusion(bf16[1024,1920]{1,0:T(8,128)(2,1)} %bitcast.29, bf16[1024,1920]{1,0:T(8,128)(2,1)} %bitcast.27), kind=kOutput, calls=%fused_computation.13 | convolution fusion | flops 4027580416 | bytes 9961472 | tf_op jit(solution)/shard_map/dot_general | solution.py:419
  149.1 0.0 copy-start.1
  149.1 69.6 %left.1 = bf16[2,8,64,1024]{3,2,1,0:T(8,128)(2,1)} custom-call(bf16[2,8,64,1024]{3,2,1,0:T(8,128)(2,1)} %bitcast.23), custom_call_target="tpu_custom_call" | custom-call | tf_op jit(solution)/shard_map/left/pallas_call | solution.py:205
  218.7 0.0 copy-done.1
  218.7 7.5 %convolution_convert_fusion = bf16[1024,1920]{1,0:T(8,128)(2,1)} fusion(bf16[1024,1024]{1,0:T(8,128)(2,1)} %bitcast.20, bf16[1024,1920]{1,0:T(8,128)(2,1)S(1)} %bitcast.28), kind=kOutput, calls=%fused_computation.12 | convolution fusion | flops 4028497920 | bytes 9961472 | tf_op jit(solution)/shard_map/dot_general | solution.py:421
  226.2 0.0 copy-start
  226.2 232.6 %right.1 = (bf16[4,2,128,7680]{3,2,1,0:T(8,128)(2,1)}, f32[2,4,8,128]{3,2,1,0:T(8,128)}) custom-call(bf16[4,2,128,1920]{3,2,1,0:T(8,128)(2,1)} %bitcast.19), custom_call_target="tpu_custom_call" | custom-call | tf_op jit(solution)/shard_map/right/pallas_call | solution.py:376
  458.8 0.0 copy-done
  458.8 16.3 %fusion.10 = f32[256,7392]{1,0:T(8,128)} fusion(bf16[1024,7680]{1,0:T(8,128)(2,1)} %bitcast.16, f32[256,7392]{1,0:T(8,128)} %copy.13, bf16[256,7392]{1,0:T(8,128)(2,1)} %copy.12, bf16[1024,1024]{1,0:T(8,128)(2,1)S(1)} %bitcast.21, s32[]{:T(128)S(6)} %select_n.35), kind=kOutput, calls=%fused_computation.7 | convolution fusion | flops 3883106304 | bytes 34701316 | tf_op jit(solution)/shard_map/dot_general | solution.py:428
  475.1 8.7 %copy.18 = f32[256,7392]{0,1:T(8,128)} copy(f32[256,7392]{1,0:T(8,128)} %fusion.10) | data formatting | bytes 15138816
  483.8 0.8 slice.13
  484.6 0.6 gather_fusion
  485.1 0.1 sqrt_bitcast_fusion
  485.2 13.4 %fusion.13 = bf16[256,7392]{0,1:T(8,128)(2,1)} fusion(bf16[1024,7680]{1,0:T(8,128)(2,1)} %bitcast.17, f32[1024]{0:T(1024)S(1)} %bitcast.25, bf16[1024,1024]{1,0:T(8,128)(2,1)S(1)} %bitcast.22, s32[]{:T(128)S(6)} %select_n.35), kind=kOutput, calls=%fused_computation.8 | convolution fusion | flops 3880108032 | bytes 19517444 | tf_op jit(solution)/shard_map/dot_general | solution.py:429
  498.6 1.6 constant_dynamic-slice_fusion
  500.3 2.3 copy.21
  502.6 0.1 dynamic_slice.11
  502.6 3.1 divide_convert_fusion
  (4 shorter events, 0.0 us)
Async XLA Ops:
  149.1 69.6 %copy-start.1 = (bf16[4,256,1920]{2,1,0:T(8,128)(2,1)S(1)}, bf16[4,256,1920]{2,1,0:T(8,128)(2,1)}, u32[]{:S(2)}) copy-start(bf16[4,256,1920]{2,1,0:T(8,128)(2,1)} %get-tuple-element.8) | copy-start | bytes 11796484
  226.2 232.6 %copy-start = (bf16[2,8,64,1024]{3,2,1,0:T(8,128)(2,1)S(1)}, bf16[2,8,64,1024]{3,2,1,0:T(8,128)(2,1)}, u32[]{:S(2)}) copy-start(bf16[2,8,64,1024]{3,2,1,0:T(8,128)(2,1)} %left.1) | copy-start | bytes 6291460

commit v2 on v1

--- a/solution.py
+++ b/solution.py
@@ -243,7 +243,8 @@
         g = lax.rem(me_o * n_col + col + k, members)
         mates.append(((g // n_col) * n_in + me_i, lax.rem(g, n_col)))
     greet(peers[1:] + mates[1:])
-    first = list(range(n_out // 2))
+    first = list(range(n_out - n_out // 2, n_out))
+    early = list(range(n_out - n_out // 2))
 
     def slot(p, i, o):
         return full_ref.at[p, i, :, pl.ds(pl.multiple_of(o * width, LANES), width)]
@@ -296,7 +297,7 @@
         copy = remote(squares, squares_got.at[k], s2.at[k], r2.at[k], mates[k])
         copy.start()
         pooled.append(copy)
-    for p in first:
+    def enter(p):
         for j in range(1, n_in):
             piece = slot(p, origin[j], me_o)
             across(j, p, 0, piece, piece).wait_recv()
@@ -304,23 +305,32 @@
                 @pl.when(can_send(way))
                 def _():
                     along(way, j, p, 1, piece, piece).start()
+
+    def onward(d, p, s):
+        for way in range(2):
+            o, there = came(way, d)
+
+            @pl.when(there)
+            def _():
+                piece = slot(p, origin[s], o)
+                along(way, s, p, d, piece, piece).wait_recv()
+                if d < n_out - 1:
+                    @pl.when(can_send(way))
+                    def _():
+                        along(way, s, p, d + 1, piece, piece).start()
+                if p not in first:
+                    for j in range(1, n_in):
+                        across(j, p, mark(way, d), piece, piece).start()
+
+    for p in early + first:
+        onward(1, p, 0)
+    for p in first:
+        enter(p)
     for d in range(1, n_out):
-        for p in list(range(len(first), n_out)) + first:
+        for p in early + first:
             for s in range(n_in if p in first else 1):
-                for way in range(2):
-                    o, there = came(way, d)
-
-                    @pl.when(there)
-                    def _():
-                        piece = slot(p, origin[s], o)
-                        along(way, s, p, d, piece, piece).wait_recv()
-                        if d < n_out - 1:
-                            @pl.when(can_send(way))
-                            def _():
-                                along(way, s, p, d + 1, piece, piece).start()
-                        if p not in first:
-                            for j in range(1, n_in):
-                                across(j, p, mark(way, d), piece, piece).start()
+                if d > 1 or s:
+                    onward(d, p, s)
     total = squares[...]
     for k in range(1, members):
         pooled[k - 1].wait_recv()

time: 507 us -> 507 us (level)
  no operation moved by 1% of the time
where the time goes in v2:
time: 507 us; the launch traced here: 506 us
  Pallas kernels  415 us (82%)
  matrix products  46.3 us (9%)
  local copies, waits for them, and re-layouts  35.4 us (7%)
  other arithmetic  8.12 us (2%)
    pallas_call x1, Pallas kernels, right(): pl.pallas_call(functools.partial(right_kernel, n_out, n_in, n_col), out_s...  233 us
    pallas_call x1, Pallas kernels, spread(): pl.pallas_call(functools.partial(spread_kernel, n_out, n_in), out_shape=(...  113 us
    pallas_call x1, Pallas kernels, left(): pl.pallas_call(functools.partial(left_kernel, n_out, n_in, n_col, n_core,...  69.6 us
    unnamed x9, local copies, waits for them, and re-layouts  28.7 us
    dot_general x1, matrix products, shards(): lax.dot_general(p_mine, r_sum, over, preferred_element_type=jnp.float32)  16.3 us
    dot_general x1, matrix products, shards(): lax.dot_general(p_even, r_sum, over, preferred_element_type=jnp.float32)  13.4 us

profile of v2, /device:TPU:0, one launch (start us, length us, event | category | flops | bytes accessed | tf_op | source)
XLA Modules:
  0.0 505.8 jit_solution(10121578405291694666)
XLA Ops:
  0.6 8.7 %copy.13 = f32[256,7392]{1,0:T(8,128)} copy(f32[256,7392]{0,1:T(8,128)} %param.3) | data formatting | bytes 15138816 | tf_op args[0]
  9.4 6.2 %copy.12 = bf16[256,7392]{1,0:T(8,128)(2,1)} copy(bf16[256,7392]{0,1:T(8,128)(2,1)} %param.4) | data formatting | bytes 7569408 | tf_op args[1]
  15.5 4.9 fusion.16
  20.4 2.2 pad.8.b_ref
  22.6 2.8 copy.14
  25.4 1.4 pad.9.q_ref
  26.8 113.1 %spread.1 = (bf16[4,256,1920]{2,1,0:T(8,128)(2,1)}, bf16[4,2,128,1920]{3,2,1,0:T(8,128)(2,1)}) custom-call(bf16[256,7680]{1,0:T(8,128)(2,1)} %pad.8.b_ref, bf16[128,7680]{1,0:T(8,128)(2,1)} %pad.9.q_ref), custom_call_target="tpu_custom_call" | custom-call | tf_op jit(solution)/shard_map/spread/pallas_call | solution.py:90
  139.9 9.1 %convolution_convert_fusion.1 = bf16[1024,1024]{1,0:T(8,128)(2,1)} fusion(bf16[1024,1920]{1,0:T(8,128)(2,1)} %bitcast.29, bf16[1024,1920]{1,0:T(8,128)(2,1)} %bitcast.27), kind=kOutput, calls=%fused_computation.13 | convolution fusion | flops 4027580416 | bytes 9961472 | tf_op jit(solution)/shard_map/dot_general | solution.py:429
  149.1 0.0 copy-start.1
  149.1 69.6 %left.1 = bf16[2,8,64,1024]{3,2,1,0:T(8,128)(2,1)} custom-call(bf16[2,8,64,1024]{3,2,1,0:T(8,128)(2,1)} %bitcast.23), custom_call_target="tpu_custom_call" | custom-call | tf_op jit(solution)/shard_map/left/pallas_call | solution.py:205
  218.7 0.0 copy-done.1
  218.7 7.5 %convolution_convert_fusion = bf16[1024,1920]{1,0:T(8,128)(2,1)} fusion(bf16[1024,1024]{1,0:T(8,128)(2,1)} %bitcast.20, bf16[1024,1920]{1,0:T(8,128)(2,1)S(1)} %bitcast.28), kind=kOutput, calls=%fused_computation.12 | convolution fusion | flops 4028497920 | bytes 9961472 | tf_op jit(solution)/shard_map/dot_general | solution.py:431
  226.2 0.0 copy-start
  226.2 232.6 %right.1 = (bf16[4,2,128,7680]{3,2,1,0:T(8,128)(2,1)}, f32[2,4,8,128]{3,2,1,0:T(8,128)}) custom-call(bf16[4,2,128,1920]{3,2,1,0:T(8,128)(2,1)} %bitcast.19), custom_call_target="tpu_custom_call" | custom-call | tf_op jit(solution)/shard_map/right/pallas_call | solution.py:386
  458.8 0.0 copy-done
  458.8 16.3 %fusion.10 = f32[256,7392]{1,0:T(8,128)} fusion(bf16[1024,7680]{1,0:T(8,128)(2,1)} %bitcast.16, f32[256,7392]{1,0:T(8,128)} %copy.13, bf16[256,7392]{1,0:T(8,128)(2,1)} %copy.12, bf16[1024,1024]{1,0:T(8,128)(2,1)S(1)} %bitcast.21, s32[]{:T(128)S(6)} %select_n.35), kind=kOutput, calls=%fused_computation.7 | convolution fusion | flops 3883106304 | bytes 34701316 | tf_op jit(solution)/shard_map/dot_general | solution.py:438
  475.1 8.7 %copy.18 = f32[256,7392]{0,1:T(8,128)} copy(f32[256,7392]{1,0:T(8,128)} %fusion.10) | data formatting | bytes 15138816
  483.8 0.8 slice.13
  484.6 0.6 gather_fusion
  485.1 0.1 sqrt_bitcast_fusion
  485.2 13.4 %fusion.13 = bf16[256,7392]{0,1:T(8,128)(2,1)} fusion(bf16[1024,7680]{1,0:T(8,128)(2,1)} %bitcast.17, f32[1024]{0:T(1024)S(1)} %bitcast.25, bf16[1024,1024]{1,0:T(8,128)(2,1)S(1)} %bitcast.22, s32[]{:T(128)S(6)} %select_n.35), kind=kOutput, calls=%fused_computation.8 | convolution fusion | flops 3880108032 | bytes 19517444 | tf_op jit(solution)/shard_map/dot_general | solution.py:439
  498.6 1.6 constant_dynamic-slice_fusion
  500.3 2.3 copy.21
  502.6 0.1 dynamic_slice.11
  502.6 3.1 divide_convert_fusion
  (4 shorter events, 0.0 us)
Async XLA Ops:
  149.1 69.6 %copy-start.1 = (bf16[4,256,1920]{2,1,0:T(8,128)(2,1)S(1)}, bf16[4,256,1920]{2,1,0:T(8,128)(2,1)}, u32[]{:S(2)}) copy-start(bf16[4,256,1920]{2,1,0:T(8,128)(2,1)} %get-tuple-element.8) | copy-start | bytes 11796484
  226.2 232.6 %copy-start = (bf16[2,8,64,1024]{3,2,1,0:T(8,128)(2,1)S(1)}, bf16[2,8,64,1024]{3,2,1,0:T(8,128)(2,1)}, u32[]{:S(2)}) copy-start(bf16[2,8,64,1024]{3,2,1,0:T(8,128)(2,1)} %left.1) | copy-start | bytes 6291460
